TPU v7x, 32 devices: a whole 2x2x4 slice. The times are simulated.
32 devices in a mesh: dp: 2 (over x), tp: 16 (over z, y, core).
Axes of the slice: x: 2, y: 2, z: 4, core: 2. Of those that a mesh axis runs over, the one named last changes fastest.
Arguments:
- hidden: bfloat16 [128, 9, 2048], P('dp'), parts along dimension 0
- norm_gain: float32 [2048], replicated
- w_head: bfloat16 [2048, 128256], P(None, 'tp')
- draft_probs: float32 [128, 8, 128256], P('dp', None, 'tp'), parts along dimension 0
- draft_tokens: int32 [128, 8], P('dp'), parts along dimension 0
- temperature: float32 [128], P('dp'), parts along dimension 0
Outputs:
- output 1: float32 [128, 8], P('dp'), parts along dimension 0
- output 2: float32 [128, 8], P('dp'), parts along dimension 0
- output 3: float32 [128, 8, 128256], P('dp', None, 'tp'), parts along dimension 0
- output 4: float32 [128], P('dp'), parts along dimension 0
There are 2 independent parts. A program takes and returns all parts, laid end to end along the dimension named above; an argument that names none is the same for every part.
All inputs are finite; a program needn't handle non-finite values.
Results may differ from a plain program's by a relative error of at most 0.001.
Values sent between devices are 32-bit elements.
A program may use at most 1 GiB of HBM per device.

v0:
```python
import jax
import jax.numpy as jnp
from jax import lax
from jax.sharding import PartitionSpec as P


def solution(mesh):
    def local_step(hidden, norm_gain, w_head, draft_probs, draft_tokens, value_a11):
        draft_len = draft_probs.shape[1]
        shard_vocab = w_head.shape[1]
        hidden_f32 = hidden.astype(jnp.float32)
        inv_rms = lax.rsqrt(jnp.mean(hidden_f32 * hidden_f32, axis=-1, keepdims=True) + 1e-5)
        normed = (hidden_f32 * inv_rms * norm_gain).astype(jnp.bfloat16)
        logits = jnp.einsum('cle,ew->clw', normed, w_head, preferred_element_type=jnp.float32)
        scaled = logits / value_a11[:, None, None]
        row_max = lax.pmax(jnp.max(scaled, axis=-1), 'tp')
        local_sum = jnp.sum(jnp.exp(scaled - row_max[:, :, None]), axis=-1)
        local_idx = draft_tokens - lax.axis_index('tp') * shard_vocab
        is_owned = (local_idx >= 0) & (local_idx < shard_vocab)
        safe_idx = jnp.clip(local_idx, 0, shard_vocab - 1)[:, :, None]
        tok_scaled = jnp.where(is_owned, jnp.take_along_axis(scaled[:, :draft_len], safe_idx, axis=-1)[:, :, 0], 0.0)
        tok_draft = jnp.where(is_owned, jnp.take_along_axis(draft_probs, safe_idx, axis=-1)[:, :, 0], 0.0)
        total_sum, tok_scaled, tok_draft = lax.psum((local_sum, tok_scaled, tok_draft), 'tp')
        row_lse = row_max + jnp.log(total_sum)
        draft_lse = row_lse[:, :draft_len]
        tok_target = jnp.exp(tok_scaled - draft_lse)
        accept = jnp.minimum(1.0, tok_target / tok_draft)
        excess = jnp.maximum(jnp.exp(scaled[:, :draft_len] - draft_lse[:, :, None]) - draft_probs, 0.0)
        norm_sum = lax.psum(jnp.sum(excess, axis=-1), 'tp')
        residual = excess / norm_sum[:, :, None]
        return accept, norm_sum, residual, row_lse[:, draft_len]

    return jax.shard_map(
        local_step,
        mesh=mesh,
        in_specs=(P('dp', None, None), P(), P(None, 'tp'), P('dp', None, 'tp'), P('dp', None), P('dp')),
        out_specs=(P('dp', None), P('dp', None), P('dp', None, 'tp'), P('dp')),
        check_vma=False,
    )
```

profile of v0, /device:TPU:0, one launch (start us, length us, event | category | flops | bytes accessed | tf_op | source)
XLA Modules:
  0.0 234.1 jit_solution(16567055087717238395)
XLA Ops:
  0.6 0.7 fusion.18
  1.4 2.2 fusion.6
  3.6 0.1 copy.24
  3.7 0.1 reshape.58
  3.8 0.0 copy-start
  3.8 0.0 copy-start.3
  3.8 0.0 copy-start.4
  3.8 8.6 %gather_fusion.1 = f32[512]{0:T(512)S(1)} fusion(f32[64,8,8016]{2,1,0:T(8,128)} %param.11, s32[512]{0:T(512)S(1)} %reshape.58), kind=kCustom, calls=%fused_computation.1.clone | custom fusion | bytes 10240 | tf_op jit(solution)/shard_map/jit(take_along_axis)/gather | solution.py:22
  12.3 0.1 reshape.67
  12.4 0.1 copy.27
  12.5 0.0 copy-done
  12.5 0.0 copy-done.3
  12.5 0.0 copy-done.4
  12.5 28.0 %fusion.19 = (f32[64,9]{0,1:T(8,128)S(1)}, f32[64,9,8016]{2,0,1:T(8,128)}) fusion(f32[64]{0:T(128)S(1)} %copy-done.4, bf16[2048,8016]{0,1:T(8,128)(2,1)} %param.10, bf16[64,9,2048]{2,0,1:T(8,128)(2,1)S(1)} %copy-done, f32[2048]{0:T(1024)S(1)} %copy-done.3, f32[64,9]{0,1:T(8,128)S(1)} %add_rsqrt_fusion), kind=kOutput, calls=%fused_computation.36 | convolution fusion | flops 18926067712 | bytes 53674752 | tf_op jit(solution)/shard_map/cle,ew->clw/dot_general | solution.py:14
  40.5 34.8 %pmax.7 = f32[64,9]{0,1:T(8,128)S(1)} all-reduce(f32[64,9]{0,1:T(8,128)S(1)} %get-tuple-element.29), channel_id=1, replica_groups=mesh['dp'=2,'tp'=16] {'tp'}, use_global_device_ids=true, to_apply=%region_3.5 | all-reduce | flops 576 | bytes 4608 | tf_op jit(solution)/shard_map/pmax | solution.py:16
  75.3 8.9 %exponential_reduce_fusion = f32[64,9]{0,1:T(8,128)S(1)} fusion(f32[64,9,8016]{2,0,1:T(8,128)} %get-tuple-element.30, f32[64,9]{0,1:T(8,128)S(1)} %pmax.7), kind=kLoop, calls=%fused_computation.4 | loop fusion | flops 9233856 | bytes 18473472 | tf_op jit(solution)/shard_map/reduce_sum | solution.py:17
  84.2 30.2 %psum.29 = f32[64,9]{0,1:T(8,128)S(1)} all-reduce(f32[64,9]{0,1:T(8,128)S(1)} %exponential_reduce_fusion), channel_id=1, replica_groups=mesh['dp'=2,'tp'=16] {'tp'}, use_global_device_ids=true, to_apply=%region_5.7 | all-reduce | flops 576 | bytes 4608 | tf_op jit(solution)/shard_map/psum | solution.py:23
  114.4 0.5 slice_bitcast_fusion
  114.9 22.1 %fusion.9 = (f32[64,8]{0,1:T(8,128)S(1)}, f32[64,8,8016]{2,0,1:T(8,128)}) fusion(f32[64,8,8016]{2,1,0:T(8,128)} %param.11, f32[64,8]{0,1:T(8,128)S(1)} %slice.29, f32[64,9,8016]{2,0,1:T(8,128)} %get-tuple-element.30), kind=kLoop, calls=%fused_computation.14 | loop fusion | flops 16416256 | bytes 49254400 | tf_op jit(solution)/shard_map/reduce_sum | solution.py:29
  137.0 0.0 copy-start.1
  137.0 8.0 %gather_fusion = f32[512]{0:T(512)S(1)} fusion(f32[64,8,8016]{2,0,1:T(8,128)} %get-tuple-element.28, s32[512]{0:T(512)S(1)} %reshape.58), kind=kCustom, calls=%fused_computation.clone | custom fusion | bytes 10240 | tf_op jit(solution)/shard_map/jit(take_along_axis)/gather | solution.py:21
  145.0 0.1 reshape.61
  145.1 0.1 copy.25
  145.2 0.0 copy-done.1
  145.2 57.6 %all-reduce = (f32[64,8]{0,1:T(8,128)S(1)}, f32[64,8]{0,1:T(8,128)S(1)}, f32[64,8]{0,1:T(8,128)S(1)}) all-reduce(f32[64,8]{0,1:T(8,128)S(1)} %bitcast_select_fusion, f32[64,8]{0,1:T(8,128)S(1)} %get-tuple-element.24, f32[64,8]{0,1:T(8,128)S(1)} %get-tuple-element.27), channel_id=1, replica_groups=mesh['dp'=2,'tp'=16] {'tp'}, use_global_device_ids=true, to_apply=%region_6.8 | all-reduce | flops 1536 | bytes 12288 | tf_op jit(solution)/shard_map/psum | solution.py:23
  202.9 0.0 copy-start.2
  202.9 12.7 %broadcast_divide_fusion = f32[64,8,8016]{2,0,1:T(8,128)S(1)} fusion(f32[64,8]{0,1:T(8,128)S(1)} %get-tuple-element.23, f32[64,8,8016]{2,1,0:T(8,128)} %param.11, f32[64,8]{0,1:T(8,128)S(1)} %slice.29, f32[64,9,8016]{2,0,1:T(8,128)} %get-tuple-element.30), kind=kLoop, calls=%fused_computation.8 | loop fusion | flops 16416768 | bytes 49254400 | tf_op jit(solution)/shard_map/div | solution.py:30
  215.5 0.0 copy-done.2
  215.5 18.0 %copy.29 = f32[64,8,8016]{2,1,0:T(8,128)} copy(f32[64,8,8016]{2,0,1:T(8,128)S(1)} %broadcast_divide_fusion) | data formatting | bytes 32833536
  233.5 0.6 divide_minimum_fusion
  (9 shorter events, 0.1 us)
Async XLA Ops:
  3.8 8.7 %copy-start = (bf16[64,9,2048]{2,0,1:T(8,128)(2,1)S(1)}, bf16[64,9,2048]{2,0,1:T(8,128)(2,1)}, u32[]{:S(2)}) copy-start(bf16[64,9,2048]{2,0,1:T(8,128)(2,1)} %param.8) | copy-start | bytes 7077892
  3.8 8.7 %copy-start.3 = (f32[2048]{0:T(1024)S(1)}, f32[2048]{0:T(1024)}, u32[]{:S(2)}) copy-start(f32[2048]{0:T(1024)} %param.9) | copy-start | bytes 24580
  3.8 8.7 %copy-start.4 = (f32[64]{0:T(128)S(1)}, f32[64]{0:T(128)}, u32[]{:S(2)}) copy-start(f32[64]{0:T(128)} %param.13) | copy-start | bytes 772
  137.0 8.2 %copy-start.1 = (s32[64,8]{0,1:T(8,128)S(1)}, s32[64,8]{0,1:T(8,128)}, u32[]{:S(2)}) copy-start(s32[64,8]{0,1:T(8,128)} %param.12) | copy-start | bytes 6148
  202.9 12.7 %copy-start.2 = (f32[64,8]{0,1:T(8,128)}, f32[64,8]{0,1:T(8,128)S(1)}, u32[]{:S(2)}) copy-start(f32[64,8]{0,1:T(8,128)S(1)} %get-tuple-element.23) | copy-start | bytes 6148
where the time goes:
time: 236 us; the launch traced here: 234 us
  blocking collectives  123 us (52%)
  other arithmetic  47.2 us (20%)
  local copies, waits for them, and re-layouts  35.6 us (15%)
  matrix products  28 us (12%)
    psum x2, blocking collectives, local_step(): lax.psum((local_sum, tok_scaled, tok_draft), 'tp')  87.8 us
    pmax x1, blocking collectives, local_step(): row_max = lax.pmax(jnp.max(scaled, axis=-1), 'tp')  34.8 us
    dot_general x1, matrix products, local_step(): jnp.einsum('cle,ew->clw', normed, w_head, preferred_element_type=jnp.floa...  28 us
    reduce_sum x1, other arithmetic, local_step(): norm_sum = lax.psum(jnp.sum(excess, axis=-1), 'tp')  22.1 us
    unnamed x11, local copies, waits for them, and re-layouts  18 us
    div x1, other arithmetic, local_step(): residual = excess / norm_sum[:, :, None]  12.7 us
    reduce_sum x1, other arithmetic, local_step(): local_sum = jnp.sum(jnp.exp(scaled - row_max[:, :, None]), axis=-1)  8.85 us
    gather x3, local copies, waits for them, and re-layouts, local_step(): jnp.take_along_axis(draft_probs, safe_idx, axis=-1)[:, :, 0]  8.69 us

commit v1 on v0

v1 whole, which is shorter than its diff:
```python
import functools
import math

import jax
import jax.numpy as jnp
from jax import lax
from jax.experimental import pallas as pl
from jax.experimental.pallas import tpu as pltpu
from jax.sharding import PartitionSpec as P

F32 = jnp.float32
BF16 = jnp.bfloat16
LOG2E = math.log2(math.e)
LN2 = math.log(2.0)
TILE = 512
SLOTS = 4
MESH = pl.DeviceIdType.MESH


def _main_kernel(n_dev, n_seq, draft, d_model, vocab,
                 g_ref, dt_ref, t_ref, h_hbm, w_hbm, q_hbm,
                 ex_ref, inv_ref, st_ref,
                 h_scr, x_ref, wbuf, q_scr, za, zb, c_ref, rel_ref, m_ref, s_ref,
                 az_ref, aq_ref, mt_ref, send1, send2, send3, recv1, recv2, recv3,
                 hsem, wsem, qsem, ssem1, ssem2, ssem3, rsem1, rsem2, rsem3):
    rows = n_seq * draft
    n_all = rows + n_seq
    n_tiles = pl.cdiv(vocab, TILE)
    last_w = vocab - (n_tiles - 1) * TILE
    last_k = pl.cdiv(last_w, 128)
    last_lanes = last_w - (last_k - 1) * 128
    n_blk = rows // 128
    me = lax.axis_index("tp")
    peers = [lax.rem(me + k, n_dev) for k in range(1, n_dev)]

    barrier = pltpu.get_barrier_semaphore()
    for p in peers:
        pl.semaphore_signal(barrier, inc=1, device_id={"tp": p}, device_id_type=MESH)

    def h_copy(j):
        return pltpu.make_async_copy(h_hbm.at[j], h_scr.at[j], hsem.at[j])

    def w_copy(t, width=TILE):
        slot = lax.rem(t, SLOTS) if not isinstance(t, int) else t % SLOTS
        start = t * TILE
        return pltpu.make_async_copy(
            w_hbm.at[pl.ds(start, width), :], wbuf.at[slot, pl.ds(0, width), :], wsem.at[slot])

    def q_copy(t, width=TILE):
        cols = pl.ds(t * TILE, width) if isinstance(t, int) else pl.ds(pl.multiple_of(t * TILE, TILE), width)
        return pltpu.make_async_copy(q_hbm.at[:, cols], q_scr.at[:, cols], qsem.at[t])

    def tile_copies(t):
        width = last_w if isinstance(t, int) and t == n_tiles - 1 else TILE
        return w_copy(t, width), q_copy(t, width)

    for j in range(draft + 1):
        h_copy(j).start()
    for t in range(3):
        for cp in tile_copies(t):
            cp.start()

    lane8 = lax.broadcasted_iota(jnp.int32, (8, 128), 1)

    t_row = t_ref[...]
    d_f = dt_ref[...].astype(F32)
    base = me * vocab
    lane_s = lax.broadcasted_iota(jnp.int32, (draft, n_seq), 1)
    t_all = jnp.broadcast_to(LOG2E / t_row, (draft, n_seq))
    for b in range(n_seq):
        pick = lane_s == b
        r8 = slice(b * draft, (b + 1) * draft)
        c = jnp.sum(jnp.where(pick, t_all, 0.0), axis=1, keepdims=True)
        d = jnp.sum(jnp.where(pick, d_f, 0.0), axis=1, keepdims=True)
        c_ref[r8, :] = jnp.broadcast_to(c, (draft, 128))
        loc = jnp.broadcast_to(d, (draft, 128)).astype(jnp.int32) - base
        owned = (loc >= 0) & (loc < vocab)
        rel_ref[r8, :] = jnp.where(owned, loc - lane8, -vocab)
    diag = lax.broadcasted_iota(jnp.int32, (n_seq, n_seq), 0) == lax.broadcasted_iota(jnp.int32, (n_seq, n_seq), 1)
    cb = jnp.sum(jnp.where(diag, jnp.broadcast_to(LOG2E / t_row, (n_seq, n_seq)), 0.0), axis=1, keepdims=True)
    c_ref[rows:n_all, :] = jnp.broadcast_to(cb, (n_seq, 128))

    m_ref[...] = jnp.full(m_ref.shape, -jnp.inf, F32)
    s_ref[...] = jnp.zeros(s_ref.shape, F32)
    m_ref[n_all:, :] = jnp.zeros((m_ref.shape[0] - n_all, 128), F32)
    s_ref[n_all:, :] = jnp.ones((m_ref.shape[0] - n_all, 128), F32)
    az_ref[...] = jnp.full(az_ref.shape, -jnp.inf, F32)
    aq_ref[...] = jnp.full(aq_ref.shape, -1.0, F32)

    n_lane = d_model // 128
    for j in range(draft + 1):
        h_copy(j).wait()
        acc = None
        for k in range(n_lane):
            hv = h_scr[j, :, k * 128:(k + 1) * 128].astype(F32)
            acc = hv * hv if acc is None else acc + hv * hv
        r = lax.rsqrt(jnp.sum(acc, axis=1, keepdims=True) * (1.0 / d_model) + 1e-5)
        r = jnp.broadcast_to(r, (n_seq, 128))
        for k in range(n_lane):
            cols = slice(k * 128, (k + 1) * 128)
            xv = h_scr[j, :, cols].astype(F32) * r * g_ref[:, cols]
            if j < draft:
                mt_ref[k, j * n_seq:(j + 1) * n_seq, :] = xv
            else:
                x_ref[rows:n_all, cols] = xv.astype(BF16)
    for b in range(0, n_seq, 2):
        for k in range(n_lane):
            cols = slice(k * 128, (k + 1) * 128)
            lo = mt_ref[k, pl.ds(b, draft, stride=n_seq), :]
            hi = mt_ref[k, pl.ds(b + 1, draft, stride=n_seq), :]
            x_ref[b * draft:(b + 2) * draft, cols] = jnp.concatenate([lo, hi], axis=0).astype(BF16)

    def dot(t, zref, kn=TILE // 128):
        slot = lax.rem(t, SLOTS) if not isinstance(t, int) else t % SLOTS
        w = wbuf[slot, 0:kn * 128, :]
        zref[:, 0:kn * 128] = lax.dot_general(
            x_ref[...], w, (((1,), (1,)), ((), ())), preferred_element_type=F32)

    def epilogue(t, zref, kn=TILE // 128, last=False):
        start = t * TILE
        for r in range(n_all // 8):
            rs = slice(r * 8, r * 8 + 8)
            zs = [zref[rs, k * 128:(k + 1) * 128] for k in range(kn)]
            if last:
                zs[-1] = jnp.where(lane8 < last_lanes, zs[-1], -jnp.inf)
            c = c_ref[rs, :]
            zm = functools.reduce(jnp.maximum, zs)
            m2 = zm * c
            es = [jnp.exp2(z * c - m2) for z in zs]
            st = functools.reduce(jnp.add, es)
            mo = m_ref[rs, :]
            mn = jnp.maximum(mo, m2)
            s_ref[rs, :] = s_ref[rs, :] * jnp.exp2(mo - mn) + st * jnp.exp2(m2 - mn)
            m_ref[rs, :] = mn
            if r * 8 >= rows:
                continue
            mt_ref[t, rs, :] = m2
            rel = rel_ref[rs, :]
            az, aq = az_ref[rs, :], aq_ref[rs, :]
            for k in range(kn):
                wd = 128 if not (last and k == kn - 1) else last_lanes
                if isinstance(t, int):
                    cs = pl.ds(start + k * 128, wd)
                else:
                    cs = pl.ds(pl.multiple_of(start + k * 128, 128), wd)
                if wd == 128:
                    ex_ref[rs, cs] = es[k]
                    qv = q_scr[rs, cs]
                    hit = rel == start + k * 128
                    az = jnp.where(hit, zs[k], az)
                    aq = jnp.where(hit, qv, aq)
                else:
                    ex_ref[rs, cs] = es[k][:, :wd]
                    qv = jnp.concatenate([q_scr[rs, cs], jnp.zeros((8, 128 - wd), F32)], axis=1)
                    hit = rel == start + k * 128
                    az = jnp.where(hit, zs[k], az)
                    aq = jnp.where(hit, qv, aq)
            az_ref[rs, :] = az
            aq_ref[rs, :] = aq

    w_copy(0).wait()
    dot(0, za)

    def pair(i, carry):
        t1 = 2 * i + 1
        t2 = 2 * i + 2

        @pl.when(i < (n_tiles - 2) // 2 - 1)
        def _():
            for cp in tile_copies(t1 + 2) + tile_copies(t2 + 2):
                cp.start()

        @pl.when(i == (n_tiles - 2) // 2 - 1)
        def _():
            for cp in tile_copies(n_tiles - 1):
                cp.start()

        w_copy(t1).wait()
        q_copy(t1 - 1).wait()
        w_copy(t2).wait()
        q_copy(t1).wait()
        dot(t1, zb)
        epilogue(t1 - 1, za)
        dot(t2, za)
        epilogue(t1, zb)
        return carry

    lax.fori_loop(0, (n_tiles - 2) // 2, pair, 0)
    w_copy(n_tiles - 1, last_w).wait()
    q_copy(n_tiles - 2).wait()
    q_copy(n_tiles - 1, last_w).wait()
    dot(n_tiles - 1, zb, last_k)
    epilogue(n_tiles - 2, za)
    epilogue(n_tiles - 1, zb, last_k, True)

    def exchange(src, dst, ssem, rsem):
        out = []
        for k, p in enumerate(peers):
            cp = pltpu.make_async_remote_copy(
                src_ref=src, dst_ref=dst.at[me], send_sem=ssem.at[k], recv_sem=rsem.at[me],
                device_id={"tp": p}, device_id_type=MESH)
            cp.start()
            out.append(cp)
        return out

    def finish(cps, src, dst, rsem):
        for p in peers:
            pltpu.make_async_remote_copy(
                src_ref=src, dst_ref=dst.at[p], send_sem=rsem.at[p], recv_sem=rsem.at[p],
                device_id={"tp": p}, device_id_type=MESH).wait_recv()

    def drain(cps):
        for cp in cps:
            cp.wait_send()

    def spread(row):
        return jnp.transpose(jnp.broadcast_to(row, (128, 128)))

    for i in range(n_blk + 1):
        blk = slice(i * 128, (i + 1) * 128)
        mt = jnp.transpose(m_ref[blk, :])
        st = jnp.transpose(s_ref[blk, :])
        mrow = jnp.max(mt, axis=0, keepdims=True)
        srow = jnp.sum(st * jnp.exp2(mt - mrow), axis=0, keepdims=True)
        send1[i:i + 1, :] = mrow + jnp.log(srow) * LOG2E
    send1[n_blk + 1:, :] = jnp.zeros((8 - n_blk - 1, 128), F32)
    send2[...] = jnp.zeros((8, 128), F32)
    send3[...] = jnp.zeros((8, 128), F32)

    pl.semaphore_wait(barrier, n_dev - 1)
    cps1 = exchange(send1, recv1, ssem1, rsem1)
    recv1[me] = send1[...]

    s_tok, q_tok = [], []
    for i in range(n_blk):
        blk = slice(i * 128, (i + 1) * 128)
        s_tok.append(jnp.max(jnp.transpose(az_ref[blk, :] * c_ref[blk, :]), axis=0, keepdims=True))
        q_tok.append(jnp.max(jnp.transpose(aq_ref[blk, :]), axis=0, keepdims=True))
    s_tok = jnp.concatenate(s_tok, axis=0)
    q_tok = jnp.concatenate(q_tok, axis=0)

    finish(cps1, send1, recv1, rsem1)
    parts = [recv1[i] for i in range(n_dev)]
    mx = functools.reduce(jnp.maximum, parts)
    tot = functools.reduce(jnp.add, [jnp.exp2(v - mx) for v in parts])
    lse2 = mx + jnp.log(tot) * LOG2E

    acc_loc = jnp.where(q_tok >= 0.0, jnp.minimum(1.0, jnp.exp2(s_tok - lse2[0:n_blk]) / q_tok), 0.0)
    send2[0:n_blk, :] = acc_loc
    cps2 = exchange(send2, recv2, ssem2, rsem2)
    recv2[me] = send2[...]

    for i in range(n_blk):
        m_ref[i * 128:(i + 1) * 128, :] = spread(lse2[i:i + 1, :])

    n_full = vocab // 128
    tail = vocab - n_full * 128

    def excess(r, carry):
        rs = pl.ds(pl.multiple_of(r * 8, 8), 8)
        lb = m_ref[rs, :]
        accs = [jnp.zeros((8, 128), F32) for _ in range(4)]
        for t in range(n_tiles):
            coef = jnp.exp2(mt_ref[t, rs, :] - lb)
            for k in range(TILE // 128):
                v = t * (TILE // 128) + k
                if v < n_full:
                    cs = slice(v * 128, (v + 1) * 128)
                    d = jnp.maximum(ex_ref[rs, cs] * coef - q_scr[rs, cs], 0.0)
                    ex_ref[rs, cs] = d
                    accs[k] = accs[k] + d
                elif v == n_full and tail:
                    cs = slice(v * 128, v * 128 + tail)
                    d = jnp.maximum(ex_ref[rs, cs] * coef[:, :tail] - q_scr[rs, cs], 0.0)
                    ex_ref[rs, cs] = d
                    accs[k] = accs[k] + jnp.concatenate([d, jnp.zeros((8, 128 - tail), F32)], axis=1)
        s_ref[rs, :] = (accs[0] + accs[1]) + (accs[2] + accs[3])
        return carry

    lax.fori_loop(0, rows // 8, excess, 0)
    for i in range(n_blk):
        blk = slice(i * 128, (i + 1) * 128)
        send3[i:i + 1, :] = jnp.sum(jnp.transpose(s_ref[blk, :]), axis=0, keepdims=True)
    cps3 = exchange(send3, recv3, ssem3, rsem3)
    recv3[me] = send3[...]

    finish(cps2, send2, recv2, rsem2)
    acc_all = functools.reduce(jnp.add, [recv2[i] for i in range(n_dev)])
    st_ref[16:17, :] = lse2[n_blk:n_blk + 1, :] * LN2

    def by_seq(dense, scr):
        for i in range(n_blk):
            scr[i * 128:(i + 1) * 128, :] = spread(dense[i:i + 1, :])
        out = jnp.zeros((8, 128), F32)
        for b in range(n_seq):
            out = jnp.where(lane8 == b, scr[b * draft:(b + 1) * draft, :], out)
        return out

    st_ref[0:8, :] = by_seq(acc_all, az_ref)
    finish(cps3, send3, recv3, rsem3)
    norm = functools.reduce(jnp.add, [recv3[i] for i in range(n_dev)])
    st_ref[8:16, :] = by_seq(norm, aq_ref)
    inv = 1.0 / norm[0:n_blk, :]
    for i in range(n_blk):
        inv_ref[i * 128:(i + 1) * 128, :] = spread(inv[i:i + 1, :])
    drain(cps1)
    drain(cps2)
    drain(cps3)


def _scale_kernel(n_seq, draft, vocab, ex_ref, inv_ref, st_ref,
                  acc_ref, norm_ref, res_hbm, lse_ref, buf, sem):
    rows = n_seq * draft
    step = buf.shape[1]
    n = rows // step
    slots = buf.shape[0]

    def copy(i):
        slot = lax.rem(i, slots) if not isinstance(i, int) else i % slots
        return pltpu.make_async_copy(
            buf.at[slot], res_hbm.at[pl.ds(pl.multiple_of(i * step, step), step), :], sem.at[slot])

    n_full = vocab // 128
    tail = vocab - n_full * 128

    def body(i, carry):
        slot = lax.rem(i, slots)

        @pl.when(i >= slots)
        def _():
            copy(i - slots).wait()

        for r in range(step // 8):
            rs = pl.ds(pl.multiple_of(i * step + r * 8, 8), 8)
            inv = inv_ref[rs, :]
            for v in range(n_full):
                cs = slice(v * 128, (v + 1) * 128)
                buf[slot, r * 8:r * 8 + 8, cs] = ex_ref[rs, cs] * inv
            if tail:
                cs = slice(n_full * 128, vocab)
                buf[slot, r * 8:r * 8 + 8, cs] = ex_ref[rs, cs] * inv[:, :tail]
        copy(i).start()
        return carry

    lax.fori_loop(0, n, body, 0)
    acc_ref[...] = st_ref[0:draft, 0:n_seq]
    norm_ref[...] = st_ref[8:8 + draft, 0:n_seq]
    lse_ref[...] = st_ref[16:17, 0:n_seq]
    for s in range(slots):
        copy(n - slots + s).wait()


def solution(mesh):
    n_dev = mesh.shape["tp"]

    def local_step(hidden, norm_gain, w_head, draft_probs, draft_tokens, value_a11):
        n_seq, n_pos, d_model = hidden.shape
        draft = n_pos - 1
        vocab = w_head.shape[1]
        rows = n_seq * draft
        n_all = rows + n_seq
        n_tiles = pl.cdiv(vocab, TILE)
        h = jnp.transpose(hidden, (1, 0, 2))
        w = jnp.transpose(w_head)
        q = draft_probs.reshape(rows, vocab)
        vm = pl.BlockSpec(memory_space=pltpu.VMEM)
        anyspec = pl.BlockSpec(memory_space=pl.ANY)
        dma = pltpu.SemaphoreType.DMA
        stat = pltpu.VMEM((n_all + 64, 128), F32)
        ex, inv, st = pl.pallas_call(
            functools.partial(_main_kernel, n_dev, n_seq, draft, d_model, vocab),
            out_shape=(
                pltpu.VMEM((rows, vocab), F32),
                pltpu.VMEM((rows, 128), F32),
                pltpu.VMEM((24, 128), F32),
            ),
            in_specs=[vm, vm, vm, anyspec, anyspec, anyspec],
            out_specs=(vm, vm, vm),
            scratch_shapes=[
                pltpu.VMEM((n_pos, n_seq, d_model), BF16),
                pltpu.VMEM((n_all, d_model), BF16),
                pltpu.VMEM((SLOTS, TILE, d_model), BF16),
                pltpu.VMEM((rows, vocab), F32),
                pltpu.VMEM((n_all, TILE), F32),
                pltpu.VMEM((n_all, TILE), F32),
                pltpu.VMEM((n_all, 128), F32),
                pltpu.VMEM((rows, 128), jnp.int32),
                stat, stat,
                pltpu.VMEM((rows, 128), F32),
                pltpu.VMEM((rows, 128), F32),
                pltpu.VMEM((n_tiles, rows, 128), F32),
                pltpu.VMEM((8, 128), F32),
                pltpu.VMEM((8, 128), F32),
                pltpu.VMEM((8, 128), F32),
                pltpu.VMEM((n_dev, 8, 128), F32),
                pltpu.VMEM((n_dev, 8, 128), F32),
                pltpu.VMEM((n_dev, 8, 128), F32),
                dma((n_pos,)), dma((SLOTS,)), dma((n_tiles,)),
                dma((n_dev,)), dma((n_dev,)), dma((n_dev,)),
                dma((n_dev,)), dma((n_dev,)), dma((n_dev,)),
            ],
            compiler_params=pltpu.CompilerParams(
                collective_id=0, has_side_effects=True, vmem_limit_bytes=46 * 2**20),
        )(norm_gain.reshape(1, d_model), jnp.transpose(draft_tokens), value_a11.reshape(1, n_seq), h, w, q)

        vmc = lambda a: pltpu.with_memory_space_constraint(a, pltpu.VMEM)
        acc, norm, res, lse = pl.pallas_call(
            functools.partial(_scale_kernel, n_seq, draft, vocab),
            out_shape=(
                jax.ShapeDtypeStruct((draft, n_seq), F32),
                jax.ShapeDtypeStruct((draft, n_seq), F32),
                jax.ShapeDtypeStruct((rows, vocab), F32),
                jax.ShapeDtypeStruct((1, n_seq), F32),
            ),
            in_specs=[vm, vm, vm],
            out_specs=(vm, vm, anyspec, vm),
            scratch_shapes=[pltpu.VMEM((8, 16, vocab), F32), dma((8,))],
            compiler_params=pltpu.CompilerParams(vmem_limit_bytes=16 * 2**20),
        )(vmc(ex), vmc(inv), vmc(st))
        return (jnp.transpose(acc), jnp.transpose(norm), res.reshape(n_seq, draft, vocab), lse.reshape(n_seq))

    return jax.shard_map(
        local_step,
        mesh=mesh,
        in_specs=(P('dp', None, None), P(), P(None, 'tp'), P('dp', None, 'tp'), P('dp', None), P('dp')),
        out_specs=(P('dp', None), P('dp', None), P('dp', None, 'tp'), P('dp')),
        check_vma=False,
    )
```

time: 236 us -> 53 us (0.22)
  blocking collectives: 123 us -> 0 us
  Pallas kernels: 0 us -> 52.2 us
  other arithmetic: 47.2 us -> 0 us
  local copies, waits for them, and re-layouts: 35.6 us -> 0 us
  matrix products: 28 us -> 0 us
    psum x2 -> x0, blocking collectives: 87.8 us -> none  [local_step(): lax.psum((local_sum, tok_scaled, tok_draft), 'tp')]
    pallas_call x0 -> x2, Pallas kernels: none -> 52.2 us  [the longest x1 45.8 us: local_step(): pl.pallas_call(functools.partial(_main_kernel, n_dev, n_seq, draft, d_mod...]
    pmax x1 -> x0, blocking collectives: 34.8 us -> none  [local_step(): row_max = lax.pmax(jnp.max(scaled, axis=-1), 'tp')]
    reduce_sum x3 -> x0, other arithmetic: 33.2 us -> none  [the longest x1 22.1 us: local_step(): norm_sum = lax.psum(jnp.sum(excess, axis=-1), 'tp')]
    dot_general x1 -> x0, matrix products: 28 us -> none  [local_step(): jnp.einsum('cle,ew->clw', normed, w_head, preferred_element_type=jnp.floa...]
    unnamed x11 -> x0, local copies, waits for them, and re-layouts: 18 us -> none
    gather x8 -> x0, local copies, waits for them, and re-layouts: 17 us -> none  [the longest x3 8.69 us: local_step(): jnp.take_along_axis(draft_probs, safe_idx, axis=-1)[:, :, 0]]
    div x1 -> x0, other arithmetic: 12.7 us -> none  [local_step(): residual = excess / norm_sum[:, :, None]]
where the time goes in v1:
time: 53 us; the launch traced here: 52.8 us
  Pallas kernels  52.2 us (98%)
  between operations  0.64 us (1%)
    pallas_call x1, Pallas kernels, local_step(): pl.pallas_call(functools.partial(_main_kernel, n_dev, n_seq, draft, d_mod...  45.8 us
    pallas_call x1, Pallas kernels, local_step(): pl.pallas_call(functools.partial(_scale_kernel, n_seq, draft, vocab), out...  6.43 us

profile of v1, /device:TPU:0, one launch (start us, length us, event | category | flops | bytes accessed | tf_op | source)
XLA Modules:
  0.0 52.8 jit_solution(8016460371162989951)
XLA Ops:
  0.6 45.8 %shard_map.93 = (f32[512,8016]{1,0:T(8,128)S(1)}, f32[512,128]{1,0:T(8,128)S(1)}, f32[24,128]{1,0:T(8,128)S(1)}) custom-call(f32[1,2048]{1,0:T(1,128)} %bitcast.13, s32[8,64]{1,0:T(8,128)} %bitcast.14, f32[1,64]{1,0:T(1,128)} %bitcast.15, bf16[9,64,2048]{2,1,0:T(8,128)(2,1)} %bitcast.12, bf16[8016,2048]{1,0:T(8,128)(2,1)} %bitcast.10, f32[512,8016]{1,0:T(8,128)} %bitcast.11), custom_call_target="tpu_custom_call" | custom-call | tf_op jit(solution)/shard_map/pallas_call | solution.py:370
  46.4 6.4 %shard_map.94 = (f32[8,64]{1,0:T(8,128)}, f32[8,64]{1,0:T(8,128)}, f32[512,8016]{1,0:T(8,128)}, f32[1,64]{1,0:T(1,128)}) custom-call(f32[512,8016]{1,0:T(8,128)S(1)} %get-tuple-element.11.ex_ref, f32[512,128]{1,0:T(8,128)S(1)} %get-tuple-element.12.inv_ref, f32[24,128]{1,0:T(8,128)S(1)} %get-tuple-element.13.st_ref), custom_call_target="tpu_custom_call" | custom-call | tf_op jit(solution)/shard_map/pallas_call | solution.py:407

commit v2 on v0

v2 whole, which is shorter than its diff:
```python
import functools
import math

import jax
import jax.numpy as jnp
from jax import lax
from jax.experimental import pallas as pl
from jax.experimental.pallas import tpu as pltpu
from jax.sharding import PartitionSpec as P

F32 = jnp.float32
BF16 = jnp.bfloat16
LOG2E = math.log2(math.e)
LN2 = math.log(2.0)
TILE = 512
SLOTS = 9
BODY = 4
UNROLL = 4
HALVED = 5
CHUNK = 32
MESH = pl.DeviceIdType.MESH


def _main_kernel(n_dev, n_seq, draft, d_model, vocab,
                 g_hbm, dt_hbm, t_hbm, h_hbm, w_hbm, q_hbm,
                 ex_ref, st_ref,
                 g_ref, dt_ref, t_ref, x_ref, wbuf, q_scr, za, zb, c_ref, rel_ref, m_ref, s_ref,
                 az_ref, aq_ref, mt_ref, send1, send2, send3, send4, recv1, recv2, recv3, recv4,
                 isem, hsem, wsem, qsem, ssem1, ssem2, ssem3, ssem4, rsem1, rsem2, rsem3, rsem4):
    rows = n_seq * draft
    n_all = rows + n_seq
    n_tiles = pl.cdiv(vocab, TILE)
    last_w = vocab - (n_tiles - 1) * TILE
    last_k = pl.cdiv(last_w, 128)
    last_lanes = last_w - (last_k - 1) * 128
    n_blk = rows // 128
    n_full = vocab // 128
    tail = vocab - n_full * 128
    stride = n_seq + 1
    me = lax.axis_index("tp")
    peers = [lax.rem(me + k, n_dev) for k in range(1, n_dev)]

    def h_dst(j):
        if j < draft:
            return wbuf.at[SLOTS - 1, pl.ds(j * n_seq, n_seq), :]
        return wbuf.at[SLOTS - 2, pl.ds(0, n_seq), :]

    def h_val(j, b0, nb, cols):
        if j < draft:
            return wbuf[SLOTS - 1, j * n_seq + b0:j * n_seq + b0 + nb, cols].astype(F32)
        return wbuf[SLOTS - 2, b0:b0 + nb, cols].astype(F32)

    def h_copy(j):
        return pltpu.make_async_copy(h_hbm.at[j], h_dst(j), hsem.at[j])

    def w_copy(t):
        if isinstance(t, int):
            slot, width = t % SLOTS, (last_w if t == n_tiles - 1 else TILE)
        else:
            slot, width = lax.rem(t, SLOTS), TILE
        return pltpu.make_async_copy(
            w_hbm.at[pl.ds(t * TILE, width), :], wbuf.at[slot, pl.ds(0, width), :], wsem.at[slot])

    def q_copy(t):
        if isinstance(t, int):
            cols = pl.ds(t * TILE, last_w if t == n_tiles - 1 else TILE)
        else:
            cols = pl.ds(pl.multiple_of(t * TILE, TILE), TILE)
        return pltpu.make_async_copy(q_hbm.at[:, cols], q_scr.at[:, cols], qsem.at[t])

    small = [pltpu.make_async_copy(src, dst, isem.at[i]) for i, (src, dst) in enumerate(
        ((dt_hbm, dt_ref), (t_hbm, t_ref), (g_hbm, g_ref)))]
    small[2].start()
    for j in [draft] + list(range(draft)):
        h_copy(j).start()
    w_copy(0).start()
    small[0].start()
    small[1].start()

    barrier = pltpu.get_barrier_semaphore()
    for p in peers:
        pl.semaphore_signal(barrier, inc=1, device_id={"tp": p}, device_id_type=MESH)

    lane8 = lax.broadcasted_iota(jnp.int32, (8, 128), 1)
    m_ref[...] = jnp.full(m_ref.shape, -jnp.inf, F32)
    s_ref[...] = jnp.zeros(s_ref.shape, F32)
    az_ref[...] = jnp.full(az_ref.shape, -jnp.inf, F32)
    n_lane = d_model // 128

    half_seq = n_seq // 2

    def inv_rms(j, b0, nb):
        acc = None
        for k in range(n_lane):
            hv = h_val(j, b0, nb, slice(k * 128, (k + 1) * 128))
            acc = hv * hv if acc is None else acc + hv * hv
        r = lax.rsqrt(jnp.sum(acc, axis=1, keepdims=True) * (1.0 / d_model) + 1e-5)
        return jnp.broadcast_to(r, (nb, 128))

    def normed(j, b0, nb, r):
        for k in range(n_lane):
            cols = slice(k * 128, (k + 1) * 128)
            xv = h_val(j, b0, nb, cols) * r * g_ref[:, cols]
            if j < draft:
                mt_ref[k, j * stride + b0:j * stride + b0 + nb, :] = xv
            else:
                x_ref[0:n_seq, cols] = xv.astype(BF16)

    def reorder(b0, nb):
        for b in range(b0, b0 + nb, 2):
            for k in range(n_lane):
                cols = slice(k * 128, (k + 1) * 128)
                lo = mt_ref[k, pl.ds(b, draft, stride=stride), :]
                hi = mt_ref[k, pl.ds(b + 1, draft, stride=stride), :]
                x_ref[n_seq + b * draft:n_seq + (b + 2) * draft, cols] = jnp.concatenate([lo, hi], axis=0).astype(BF16)

    def norm_some(js, b0, nb, wait=False):
        for n, j in enumerate(js):
            if n == 0:
                if wait:
                    h_copy(j).wait()
                r = inv_rms(j, b0, nb[0])
            r_next = None
            if n + 1 < len(js):
                if wait and n % 4 == 0:
                    for ahead in js[n + 1:n + 5]:
                        h_copy(ahead).wait()
                r_next = inv_rms(js[n + 1], b0, nb[n + 1])
            normed(j, b0, nb[n], r)
            r = r_next
            if wait and n == 4:
                for t in range(1, SLOTS - 2):
                    w_copy(t).start()

    small[2].wait()
    norm_some([draft] + list(range(draft)), 0, [n_seq] + [half_seq] * draft, True)
    reorder(0, half_seq)

    def dot(t, zref, part):
        kn = last_k if isinstance(t, int) and t == n_tiles - 1 else TILE // 128
        slot = lax.rem(t, SLOTS) if not isinstance(t, int) else t % SLOTS
        zref[part, 0:kn * 128] = lax.dot_general(
            x_ref[part, :], wbuf[slot, 0:kn * 128, :], (((1,), (1,)), ((), ())), preferred_element_type=F32)

    lane_c = lax.broadcasted_iota(jnp.int32, (CHUNK, 128), 1)

    def pick_z(t, row, zs):
        rs = slice(row, row + CHUNK)
        rel, az = rel_ref[rs, :], az_ref[rs, :]
        for k, z in enumerate(zs):
            az = jnp.where(rel == t * TILE + k * 128, z, az)
        az_ref[rs, :] = az

    def epilogue(t, zref, part, pick=True):
        last = isinstance(t, int) and t == n_tiles - 1
        kn = last_k if last else TILE // 128
        for row in range(part.start, part.stop, CHUNK):
            rs = slice(row, row + CHUNK)
            zs = [zref[rs, k * 128:(k + 1) * 128] for k in range(kn)]
            if last:
                zs[-1] = jnp.where(lane_c < last_lanes, zs[-1], -jnp.inf)
            c = c_ref[rs, :]
            m2 = functools.reduce(jnp.maximum, zs) * c
            es = [jnp.exp2(z * c - m2) for z in zs]
            st = functools.reduce(jnp.add, es)
            mo = m_ref[rs, :]
            mn = jnp.maximum(mo, m2)
            s_ref[rs, :] = s_ref[rs, :] * jnp.exp2(mo - mn) + st * jnp.exp2(m2 - mn)
            m_ref[rs, :] = mn
            if row < n_seq:
                continue
            rs = slice(row - n_seq, row - n_seq + CHUNK)
            mt_ref[t, rs, :] = m2
            for k in range(kn):
                wd = 128 if not (last and k == kn - 1) else last_lanes
                cs = pl.ds(t * TILE + k * 128, wd)
                if not isinstance(t, int):
                    cs = pl.ds(pl.multiple_of(t * TILE + k * 128, 128), wd)
                ex_ref[rs, cs] = es[k] if wd == 128 else es[k][:, :wd]
            if pick:
                pick_z(t, row - n_seq, zs)

    zbuf = (za, zb)
    whole = slice(0, n_all)
    half1 = slice(0, n_seq + rows // 2)
    half2 = slice(n_seq + rows // 2, n_all)

    def step(ts, prev):
        for t, zref in ts:
            dot(t, zref, whole)
            epilogue(*prev, whole)
            prev = (t, zref)

    small[0].wait()
    small[1].wait()
    w_copy(0).wait()
    dot(0, za, half1)
    norm_some(list(range(draft)), half_seq, [half_seq] * draft)
    reorder(half_seq, half_seq)
    t_row = t_ref[...]
    d_f = dt_ref[...].astype(F32)
    base = me * vocab
    lane_s = lax.broadcasted_iota(jnp.int32, (draft, n_seq), 1)
    t_all = jnp.broadcast_to(LOG2E / t_row, (draft, n_seq))
    for b in range(n_seq):
        pick = lane_s == b
        r8 = slice(b * draft, (b + 1) * draft)
        c = jnp.sum(jnp.where(pick, t_all, 0.0), axis=1, keepdims=True)
        d = jnp.sum(jnp.where(pick, d_f, 0.0), axis=1, keepdims=True)
        c_ref[n_seq + b * draft:n_seq + (b + 1) * draft, :] = jnp.broadcast_to(c, (draft, 128))
        loc = jnp.broadcast_to(d, (draft, 128)).astype(jnp.int32) - base
        owned = (loc >= 0) & (loc < vocab)
        rel_ref[r8, :] = jnp.where(owned, loc - lane8, -vocab)
    diag = lax.broadcasted_iota(jnp.int32, (n_seq, n_seq), 0) == lax.broadcasted_iota(jnp.int32, (n_seq, n_seq), 1)
    cb = jnp.sum(jnp.where(diag, jnp.broadcast_to(LOG2E / t_row, (n_seq, n_seq)), 0.0), axis=1, keepdims=True)
    c_ref[0:n_seq, :] = jnp.broadcast_to(cb, (n_seq, 128))

    dot(0, za, half2)
    w_copy(SLOTS - 2).start()
    w_copy(SLOTS - 1).start()
    for t in range(6):
        q_copy(t).start()
    w_copy(1).wait()
    w_copy(2).wait()
    step([(1, zb), (2, za)], (0, za))
    first = n_tiles - HALVED
    n_body = (first - 3) // BODY

    def body(i, carry):
        t = BODY * i + 3
        for u in range(BODY):
            w_copy(t + u).wait()

        @pl.when(i == 0)
        def _():
            for u in range(SLOTS, SLOTS + 3):
                w_copy(u).start()
            for u in range(6, 10):
                q_copy(u).start()

        @pl.when(i == 1)
        def _():
            for u in range(SLOTS + 3, n_tiles):
                w_copy(u).start()
            for u in range(10, n_tiles):
                q_copy(u).start()

        step([(t + u, zbuf[(u + 1) % 2]) for u in range(BODY)], (t - 1, za))
        return carry

    lax.fori_loop(0, n_body, body, 0)
    for t in range(first, n_tiles):
        w_copy(t).wait()
    prev = (first - 1, za, whole)
    u = 1
    for t in range(first, n_tiles):
        dot(t, zbuf[u], half1)
        epilogue(*prev)
        prev = (t, zbuf[u], half1)
        u = 1 - u

    def exchange(src, dst, ssem, rsem):
        out = []
        for k, p in enumerate(peers):
            cp = pltpu.make_async_remote_copy(
                src_ref=src, dst_ref=dst.at[me], send_sem=ssem.at[k], recv_sem=rsem.at[me],
                device_id={"tp": p}, device_id_type=MESH)
            cp.start()
            out.append(cp)
        return out

    def finish(src, dst, rsem):
        for p in peers:
            pltpu.make_async_remote_copy(
                src_ref=src, dst_ref=dst.at[p], send_sem=rsem.at[p], recv_sem=rsem.at[p],
                device_id={"tp": p}, device_id_type=MESH).wait_recv()

    def drain(cps):
        for cp in cps:
            cp.wait_send()

    def spread(row):
        return jnp.transpose(jnp.broadcast_to(row, (128, 128)))

    def log_sum(start):
        blk = slice(start, start + 128)
        mt = jnp.transpose(m_ref[blk, :])
        st = jnp.transpose(s_ref[blk, :])
        mrow = jnp.max(mt, axis=0, keepdims=True)
        return mrow + jnp.log(jnp.sum(st * jnp.exp2(mt - mrow), axis=0, keepdims=True)) * LOG2E

    def log_total(recv):
        parts = [recv[i] for i in range(n_dev)]
        mx = functools.reduce(jnp.maximum, parts)
        return mx + jnp.log(functools.reduce(jnp.add, [jnp.exp2(v - mx) for v in parts])) * LOG2E

    hb = n_blk // 2

    def first_half():
        for i in range(hb):
            send1[i:i + 1, :] = log_sum(n_seq + i * 128)
        send1[hb:hb + 1, :] = log_sum(0)
        pl.semaphore_wait(barrier, n_dev - 1)
        cps1 = exchange(send1, recv1, ssem1, rsem1)
        recv1[me] = send1[...]
        return cps1

    for t in range(first, n_tiles):
        dot(t, zbuf[u], half2)
        epilogue(*prev)
        prev = (t, zbuf[u], half2)
        u = 1 - u
        if t == n_tiles - 4:
            cps1 = first_half()
    if HALVED < 4:
        cps1 = first_half()
    epilogue(*prev, pick=False)
    for i in range(hb, n_blk):
        send2[i - hb:i - hb + 1, :] = log_sum(n_seq + i * 128)
    cps2 = exchange(send2, recv2, ssem2, rsem2)
    recv2[me] = send2[...]

    for row in range(half2.start, half2.stop, CHUNK):
        rs = slice(row, row + CHUNK)
        pick_z(n_tiles - 1, row - n_seq, [prev[1][rs, k * 128:(k + 1) * 128] for k in range(last_k)])
    for t in range(n_tiles):
        q_copy(t).wait()

    def pick_q(i, carry):
        rs = pl.ds(pl.multiple_of(i * 16, 16), 16)
        rel = rel_ref[rs, :]
        aqs = [jnp.full((16, 128), -1.0, F32) for _ in range(4)]
        for v in range(n_full):
            aqs[v % 4] = jnp.where(rel == v * 128, q_scr[rs, v * 128:(v + 1) * 128], aqs[v % 4])
        if tail:
            qv = jnp.concatenate(
                [q_scr[rs, n_full * 128:vocab], jnp.zeros((16, 128 - tail), F32)], axis=1)
            aqs[0] = jnp.where(rel == n_full * 128, qv, aqs[0])
        aq_ref[rs, :] = functools.reduce(jnp.maximum, aqs)
        return carry

    lax.fori_loop(0, rows // 16, pick_q, 0)
    s_tok, q_tok = [], []
    for i in range(n_blk):
        blk = slice(i * 128, (i + 1) * 128)
        s_tok.append(jnp.max(jnp.transpose(az_ref[blk, :] * c_ref[n_seq + i * 128:n_seq + (i + 1) * 128, :]), axis=0, keepdims=True))
        q_tok.append(jnp.max(jnp.transpose(aq_ref[blk, :]), axis=0, keepdims=True))
    s_tok = jnp.concatenate(s_tok, axis=0)
    q_tok = jnp.concatenate(q_tok, axis=0)

    def excess(i, carry):
        n = 8 * UNROLL
        rs = pl.ds(pl.multiple_of(i * n, n), n)
        rz = pl.ds(pl.multiple_of(i * n + n_seq, 8), n)
        lb = m_ref[rz, :]
        accs = [jnp.zeros((n, 128), F32) for _ in range(2)]
        for t in range(n_tiles):
            coef = jnp.exp2(mt_ref[t, rs, :] - lb)
            for k in range(TILE // 128):
                v = t * (TILE // 128) + k
                if v < n_full:
                    cs = slice(v * 128, (v + 1) * 128)
                    d = jnp.maximum(ex_ref[rs, cs] * coef - q_scr[rs, cs], 0.0)
                    ex_ref[rs, cs] = d
                    accs[k % 2] = accs[k % 2] + d
                elif v == n_full and tail:
                    cs = slice(v * 128, v * 128 + tail)
                    d = jnp.maximum(ex_ref[rs, cs] * coef[:, :tail] - q_scr[rs, cs], 0.0)
                    ex_ref[rs, cs] = d
                    accs[k % 2] = accs[k % 2] + jnp.concatenate([d, jnp.zeros((n, 128 - tail), F32)], axis=1)
        s_ref[rz, :] = accs[0] + accs[1]
        return carry

    per_half = rows // (16 * UNROLL)

    def norm_part(i):
        blk = slice(n_seq + i * 128, n_seq + (i + 1) * 128)
        return jnp.sum(jnp.transpose(s_ref[blk, :]), axis=0, keepdims=True)

    finish(send1, recv1, rsem1)
    lse_a = log_total(recv1)
    for i in range(hb):
        m_ref[n_seq + i * 128:n_seq + (i + 1) * 128, :] = spread(lse_a[i:i + 1, :])
    lax.fori_loop(0, per_half, excess, 0)
    for i in range(hb):
        send3[i:i + 1, :] = norm_part(i)
    cps3 = exchange(send3, recv3, ssem3, rsem3)
    recv3[me] = send3[...]

    finish(send2, recv2, rsem2)
    lse_b = log_total(recv2)
    for i in range(hb, n_blk):
        m_ref[n_seq + i * 128:n_seq + (i + 1) * 128, :] = spread(lse_b[i - hb:i - hb + 1, :])
    lax.fori_loop(per_half, 2 * per_half, excess, 0)
    for i in range(hb, n_blk):
        send4[i - hb:i - hb + 1, :] = norm_part(i)
    lse = jnp.concatenate([lse_a[0:hb], lse_b[0:n_blk - hb]], axis=0)
    acc = jnp.where(q_tok >= 0.0, jnp.minimum(1.0, jnp.exp2(s_tok - lse) / q_tok), 0.0)
    send4[n_blk - hb:2 * n_blk - hb, :] = acc
    cps4 = exchange(send4, recv4, ssem4, rsem4)
    recv4[me] = send4[...]
    st_ref[2 * n_blk:2 * n_blk + 1, :] = lse_a[hb:hb + 1, :] * LN2

    drain(cps1 + cps2 + cps3)
    finish(send3, recv3, rsem3)
    st_ref[0:hb, :] = functools.reduce(jnp.add, [recv3[i] for i in range(n_dev)])
    finish(send4, recv4, rsem4)
    st_ref[hb:2 * n_blk, :] = functools.reduce(jnp.add, [recv4[i] for i in range(n_dev)])
    drain(cps4)


def _scale_kernel(n_seq, draft, vocab, ex_ref, st_ref,
                  acc_hbm, norm_hbm, res_hbm, lse_hbm, acc_ref, norm_ref, lse_ref, nb_ref, ab_ref, buf, sem, osem):
    rows = n_seq * draft
    step = buf.shape[1]
    n = rows // step
    slots = buf.shape[0]
    lane8 = lax.broadcasted_iota(jnp.int32, (8, 128), 1)

    def copy(i):
        slot = lax.rem(i, slots) if not isinstance(i, int) else i % slots
        return pltpu.make_async_copy(
            buf.at[slot], res_hbm.at[pl.ds(pl.multiple_of(i * step, step), step), :], sem.at[slot])

    n_full = vocab // 128
    tail = vocab - n_full * 128

    def body(i, carry):
        slot = lax.rem(i, slots)

        @pl.when(i >= slots)
        def _():
            copy(i - slots).wait()

        for r in range(step // 8):
            rs = pl.ds(pl.multiple_of(i * step + r * 8, 8), 8)
            inv = 1.0 / nb_ref[rs, :]
            for v in range(n_full):
                cs = slice(v * 128, (v + 1) * 128)
                buf[slot, r * 8:r * 8 + 8, cs] = ex_ref[rs, cs] * inv
            if tail:
                cs = slice(n_full * 128, vocab)
                buf[slot, r * 8:r * 8 + 8, cs] = ex_ref[rs, cs] * inv[:, :tail]
        copy(i).start()
        return carry

    n_blk = rows // 128

    def spread(dst, row):
        for i in range(n_blk):
            dst[i * 128:(i + 1) * 128, :] = jnp.transpose(
                jnp.broadcast_to(st_ref[row + i:row + i + 1, :], (128, 128)))

    def by_seq(src):
        out = jnp.zeros((8, 128), F32)
        for b in range(n_seq):
            out = jnp.where(lane8 == b, src[b * draft:(b + 1) * draft, :], out)
        return out[0:draft, 0:n_seq]

    spread(nb_ref, 0)
    lax.fori_loop(0, slots, body, 0)
    spread(ab_ref, n_blk)
    acc_ref[...] = by_seq(ab_ref)
    norm_ref[...] = by_seq(nb_ref)
    lse_ref[...] = st_ref[2 * n_blk:2 * n_blk + 1, 0:n_seq]
    outs = [pltpu.make_async_copy(src, dst, osem.at[i]) for i, (src, dst) in enumerate(
        ((acc_ref, acc_hbm), (norm_ref, norm_hbm), (lse_ref, lse_hbm)))]
    for cp in outs:
        cp.start()
    lax.fori_loop(slots, n, body, 0)
    for cp in outs:
        cp.wait()
    for s in range(slots):
        copy(n - slots + s).wait()


def solution(mesh):
    n_dev = mesh.shape["tp"]

    def local_step(hidden, norm_gain, w_head, draft_probs, draft_tokens, value_a11):
        n_seq, n_pos, d_model = hidden.shape
        draft = n_pos - 1
        vocab = w_head.shape[1]
        rows = n_seq * draft
        n_all = rows + n_seq
        n_tiles = pl.cdiv(vocab, TILE)
        h = jnp.transpose(hidden, (1, 0, 2))
        w = jnp.transpose(w_head)
        q = draft_probs.reshape(rows, vocab)
        vm = pl.BlockSpec(memory_space=pltpu.VMEM)
        anyspec = pl.BlockSpec(memory_space=pl.ANY)
        dma = pltpu.SemaphoreType.DMA
        stat = pltpu.VMEM((n_all, 128), F32)
        n_blk = rows // 128
        msgs = (n_blk // 2 + 1, n_blk - n_blk // 2, n_blk // 2, 2 * n_blk - n_blk // 2)
        ex, st = pl.pallas_call(
            functools.partial(_main_kernel, n_dev, n_seq, draft, d_model, vocab),
            out_shape=(
                pltpu.VMEM((rows, vocab), F32),
                pltpu.VMEM((2 * n_blk + 8, 128), F32),
            ),
            in_specs=[anyspec] * 6,
            out_specs=(vm, vm),
            scratch_shapes=[
                pltpu.VMEM((1, d_model), F32),
                pltpu.VMEM((draft, n_seq), jnp.int32),
                pltpu.VMEM((1, n_seq), F32),
                pltpu.VMEM((n_all, d_model), BF16),
                pltpu.VMEM((SLOTS, TILE, d_model), BF16),
                pltpu.VMEM((rows, vocab), F32),
                pltpu.VMEM((n_all, TILE), F32),
                pltpu.VMEM((n_all, TILE), F32),
                pltpu.VMEM((n_all, 128), F32),
                pltpu.VMEM((rows, 128), jnp.int32),
                stat, stat,
                pltpu.VMEM((rows, 128), F32),
                pltpu.VMEM((rows, 128), F32),
                pltpu.VMEM((n_tiles, rows + 8, 128), F32),
                *[pltpu.VMEM((m, 128), F32) for m in msgs],
                *[pltpu.VMEM((n_dev, m, 128), F32) for m in msgs],
                dma((3,)), dma((n_pos,)), dma((SLOTS,)), dma((n_tiles,)),
                *[dma((n_dev,)) for _ in range(8)],
            ],
            compiler_params=pltpu.CompilerParams(
                collective_id=0, has_side_effects=True, vmem_limit_bytes=48 * 2**20),
        )(norm_gain.reshape(1, d_model), jnp.transpose(draft_tokens), value_a11.reshape(1, n_seq), h, w, q)

        vmc = lambda a: pltpu.with_memory_space_constraint(a, pltpu.VMEM)
        acc, norm, res, lse = pl.pallas_call(
            functools.partial(_scale_kernel, n_seq, draft, vocab),
            out_shape=(
                jax.ShapeDtypeStruct((draft, n_seq), F32),
                jax.ShapeDtypeStruct((draft, n_seq), F32),
                jax.ShapeDtypeStruct((rows, vocab), F32),
                jax.ShapeDtypeStruct((1, n_seq), F32),
            ),
            in_specs=[vm, vm],
            out_specs=(anyspec,) * 4,
            scratch_shapes=[
                pltpu.VMEM((draft, n_seq), F32), pltpu.VMEM((draft, n_seq), F32), pltpu.VMEM((1, n_seq), F32),
                pltpu.VMEM((rows, 128), F32), pltpu.VMEM((rows, 128), F32),
                pltpu.VMEM((8, 16, vocab), F32), dma((8,)), dma((3,)),
            ],
            compiler_params=pltpu.CompilerParams(vmem_limit_bytes=16 * 2**20),
        )(vmc(ex), vmc(st))
        return (jnp.transpose(acc), jnp.transpose(norm), res.reshape(n_seq, draft, vocab), lse.reshape(n_seq))

    return jax.shard_map(
        local_step,
        mesh=mesh,
        in_specs=(P('dp', None, None), P(), P(None, 'tp'), P('dp', None, 'tp'), P('dp', None), P('dp')),
        out_specs=(P('dp', None), P('dp', None), P('dp', None, 'tp'), P('dp')),
        check_vma=False,
    )
```

time: 236 us -> 46.5 us (0.20)
  blocking collectives: 123 us -> 0 us
  other arithmetic: 47.2 us -> 0 us
  Pallas kernels: 0 us -> 45.5 us
  local copies, waits for them, and re-layouts: 35.6 us -> 0 us
  matrix products: 28 us -> 0 us
    psum x2 -> x0, blocking collectives: 87.8 us -> none  [local_step(): lax.psum((local_sum, tok_scaled, tok_draft), 'tp')]
    pallas_call x0 -> x2, Pallas kernels: none -> 45.5 us  [the longest x1 39.5 us: local_step(): pl.pallas_call(functools.partial(_main_kernel, n_dev, n_seq, draft, d_mod...]
    pmax x1 -> x0, blocking collectives: 34.8 us -> none  [local_step(): row_max = lax.pmax(jnp.max(scaled, axis=-1), 'tp')]
    reduce_sum x3 -> x0, other arithmetic: 33.2 us -> none  [the longest x1 22.1 us: local_step(): norm_sum = lax.psum(jnp.sum(excess, axis=-1), 'tp')]
    dot_general x1 -> x0, matrix products: 28 us -> none  [local_step(): jnp.einsum('cle,ew->clw', normed, w_head, preferred_element_type=jnp.floa...]
    unnamed x11 -> x0, local copies, waits for them, and re-layouts: 18 us -> none
    gather x8 -> x0, local copies, waits for them, and re-layouts: 17 us -> none  [the longest x3 8.69 us: local_step(): jnp.take_along_axis(draft_probs, safe_idx, axis=-1)[:, :, 0]]
    div x1 -> x0, other arithmetic: 12.7 us -> none  [local_step(): residual = excess / norm_sum[:, :, None]]
where the time goes in v2:
time: 46.5 us; the launch traced here: 46.3 us
  Pallas kernels  45.5 us (98%)
  between operations  0.8 us (2%)
    pallas_call x1, Pallas kernels, local_step(): pl.pallas_call(functools.partial(_main_kernel, n_dev, n_seq, draft, d_mod...  39.5 us
    pallas_call x1, Pallas kernels, local_step(): pl.pallas_call(functools.partial(_scale_kernel, n_seq, draft, vocab), out...  6 us

profile of v2, /device:TPU:0, one launch (start us, length us, event | category | flops | bytes accessed | tf_op | source)
XLA Modules:
  0.0 46.3 jit_solution(3646845618299517511)
XLA Ops:
  0.6 39.5 %shard_map.93 = (f32[512,8016]{1,0:T(8,128)S(1)}, f32[16,128]{1,0:T(8,128)S(1)}) custom-call(f32[1,2048]{1,0:T(1,128)} %bitcast.13, s32[8,64]{1,0:T(8,128)} %bitcast.14, f32[1,64]{1,0:T(1,128)} %bitcast.15, bf16[9,64,2048]{2,1,0:T(8,128)(2,1)} %bitcast.12, bf16[8016,2048]{1,0:T(8,128)(2,1)} %bitcast.10, f32[512,8016]{1,0:T(8,128)} %bitcast.11), custom_call_target="tpu_custom_call" | custom-call | tf_op jit(solution)/shard_map/pallas_call | solution.py:496
  40.1 6.0 %shard_map.94 = (f32[8,64]{1,0:T(8,128)}, f32[8,64]{1,0:T(8,128)}, f32[512,8016]{1,0:T(8,128)}, f32[1,64]{1,0:T(1,128)}) custom-call(f32[512,8016]{1,0:T(8,128)S(1)} %get-tuple-element.10.ex_ref, f32[16,128]{1,0:T(8,128)S(1)} %get-tuple-element.11.st_ref), custom_call_target="tpu_custom_call" | custom-call | tf_op jit(solution)/shard_map/pallas_call | solution.py:529
